TPU v7x, 64 devices: a 2x2x8 block of a 4x4x8 slice. The times are simulated.
64 devices in a mesh: dp: 4 (over x, y), sp: 16 (over z, core).
Axes of the slice: x: 2, y: 2, z: 8, core: 2. Of those that a mesh axis runs over, the one named last changes fastest.
The devices are a block of a 4x4x8 slice.
Arguments:
- resid_x: bfloat16 [32, 2048, 2048], P('dp', 'sp'), parts along dimension 0
- positions: int32 [32, 2048], P('dp', 'sp'), parts along dimension 0
- w_query: bfloat16 [2048, 2048], replicated
- w_key: bfloat16 [2048, 2048], replicated
- w_value: bfloat16 [2048, 2048], replicated
- w_out: bfloat16 [2048, 2048], replicated
- gain_q: bfloat16 [2048], replicated
- gain_k: bfloat16 [2048], replicated
- gain_out: bfloat16 [2048], replicated
Outputs:
- output: bfloat16 [32, 2048, 2048], P('dp', 'sp'), parts along dimension 0
There are 4 independent parts. A program takes and returns all parts, laid end to end along the dimension named above; an argument that names none is the same for every part.
All inputs are finite; a program needn't handle non-finite values.
Results may differ from a plain program's by a relative error of at most 0.0186704.
Values are sent between devices in bfloat16 or wider.
A program may use at most 768 MiB of HBM per device.

v0:
```python
import jax
import jax.numpy as jnp
from jax import lax
from jax.sharding import PartitionSpec as P

HEAD_DIM = 128
QUERY_BLOCKS = 8
ROPE_THETA = 500000.0
NORM_EPS = 1e-6
SCALE = HEAD_DIM ** -0.5


def rope_tables(pos_ids):
    inv_freq = 1.0 / (ROPE_THETA ** (jnp.arange(0, HEAD_DIM, 2, dtype=jnp.float32) / HEAD_DIM))
    angles = pos_ids.astype(jnp.float32)[..., None] * inv_freq
    return jnp.cos(angles), jnp.sin(angles)


def apply_rope(heads_f32, cos_t, sin_t):
    half = HEAD_DIM // 2
    cos_b = cos_t[:, :, None, :]
    sin_b = sin_t[:, :, None, :]
    first = heads_f32[..., :half]
    second = heads_f32[..., half:]
    return jnp.concatenate([first * cos_b - second * sin_b, second * cos_b + first * sin_b], axis=-1)


def rms_scale(vals_f32, gain):
    mean_sq = jnp.mean(vals_f32 * vals_f32, axis=-1, keepdims=True)
    return vals_f32 * lax.rsqrt(mean_sq + NORM_EPS) * gain.astype(jnp.float32)


def project(x_tok, weight):
    return jnp.einsum('bsd,de->bse', x_tok, weight, preferred_element_type=jnp.float32).astype(jnp.bfloat16)


def norm_rope(x_tok, weight, gain, cos_t, sin_t):
    proj = project(x_tok, weight).astype(jnp.float32)
    batch, seq_len, model_width = proj.shape
    normed = rms_scale(proj, gain).reshape(batch, seq_len, model_width // HEAD_DIM, HEAD_DIM)
    return apply_rope(normed, cos_t, sin_t).astype(jnp.bfloat16)


def causal_attention(q_heads, k_heads, v_heads):
    seq_len = q_heads.shape[1]
    block = seq_len // QUERY_BLOCKS
    outs = []
    for blk_idx in range(QUERY_BLOCKS):
        key_end = (blk_idx + 1) * block
        q_blk = q_heads[:, blk_idx * block:key_end]
        scores = jnp.einsum('bqhd,bkhd->bhqk', q_blk, k_heads[:, :key_end], preferred_element_type=jnp.float32) * SCALE
        q_idx = blk_idx * block + jnp.arange(block)
        scores = jnp.where(jnp.arange(key_end)[None, :] <= q_idx[:, None], scores, -1e30)
        probs = jax.nn.softmax(scores, axis=-1).astype(jnp.bfloat16)
        outs.append(jnp.einsum('bhqk,bkhd->bqhd', probs, v_heads[:, :key_end], preferred_element_type=jnp.float32).astype(jnp.bfloat16))
    return jnp.concatenate(outs, axis=1)


def solution(mesh):
    def local_block(x_loc, pos_loc, w_query, w_key, w_value, w_out, gain_q, gain_k, gain_out):
        batch, seq_loc, model_width = x_loc.shape
        cos_t, sin_t = rope_tables(pos_loc)
        q_loc = norm_rope(x_loc, w_query, gain_q, cos_t, sin_t)
        k_loc = norm_rope(x_loc, w_key, gain_k, cos_t, sin_t)
        v_loc = project(x_loc, w_value).reshape(batch, seq_loc, model_width // HEAD_DIM, HEAD_DIM)
        q_heads = lax.all_to_all(q_loc, 'sp', 2, 1, tiled=True)
        k_heads = lax.all_to_all(k_loc, 'sp', 2, 1, tiled=True)
        v_heads = lax.all_to_all(v_loc, 'sp', 2, 1, tiled=True)
        o_heads = causal_attention(q_heads, k_heads, v_heads)
        o_loc = lax.all_to_all(o_heads, 'sp', 1, 2, tiled=True).reshape(batch, seq_loc, model_width)
        attn_out = project(o_loc, w_out).astype(jnp.float32)
        return (x_loc.astype(jnp.float32) + rms_scale(attn_out, gain_out)).astype(jnp.bfloat16)

    tok_spec = P('dp', 'sp', None)
    return jax.shard_map(local_block, mesh=mesh, in_specs=(tok_spec, P('dp', 'sp'), P(), P(), P(), P(), P(), P(), P()), out_specs=tok_spec, check_vma=False)
```

profile of v0, /device:TPU:21, one launch (start us, length us, event | category | flops | bytes accessed | tf_op | source)
XLA Modules:
  0.0 705.9 jit_solution(7008956571894854639)
XLA Ops:
  0.0 0.7 convert_element_type.149
  0.7 12.6 %fusion.12 = (f32[8,128]{1,0:T(8,128)S(1)}, bf16[8,128,2048]{2,1,0:T(8,128)(2,1)S(1)}) fusion(bf16[8,128,2048]{2,1,0:T(8,128)(2,1)} %param.9, bf16[2048,2048]{1,0:T(8,128)(2,1)} %param.11), kind=kOutput, calls=%fused_computation.30 | convolution fusion | flops 8598322176 | bytes 16781312 | tf_op jit(solution)/shard_map/bsd,de->bse/dot_general | solution.py:34
  13.3 0.9 fusion.13
  14.2 2.0 copy.36
  16.3 13.2 %fusion.14 = (f32[8,128]{1,0:T(8,128)S(1)}, bf16[8,128,2048]{2,1,0:T(8,128)(2,1)S(1)}) fusion(bf16[8,128,2048]{2,1,0:T(8,128)(2,1)} %param.9, bf16[2048,2048]{1,0:T(8,128)(2,1)} %param.12), kind=kOutput, calls=%fused_computation.32 | convolution fusion | flops 8598322176 | bytes 16781312 | tf_op jit(solution)/shard_map/bsd,de->bse/dot_general | solution.py:34
  29.5 0.9 fusion.15
  30.4 5.2 copy.37
  35.6 17.0 %fusion.121 = (f32[8,128,16,64]{3,2,1,0:T(8,128)}, f32[8,128,16,64]{3,2,1,0:T(8,128)}, f32[8,128,16,64]{3,2,1,0:T(8,128)}, f32[8,128,16,64]{3,2,1,0:T(8,128)}) fusion(f32[8,128,16,128]{3,2,1,0:T(8,128)S(1)} %bitcast.255, f32[8,128,16,128]{3,2,1,0:T(8,128)} %bitcast.256), kind=kLoop, calls=%fused_computation.196 | loop fusion | bytes 33554432 | tf_op jit(solution)/shard_map/slice | solution.py:23
  52.5 1.9 multiply_cosine_fusion
  54.4 30.9 %subtract_convert_fusion.1 = (bf16[8,128,16,64]{3,1,0,2:T(8,128)(2,1)}, bf16[8,128,16,64]{3,1,0,2:T(8,128)(2,1)}, bf16[8,128,16,64]{3,1,0,2:T(8,128)(2,1)}, bf16[8,128,16,64]{3,1,0,2:T(8,128)(2,1)}) fusion(f32[8,128,16,64]{3,2,1,0:T(8,128)} %get-tuple-element.10, f32[8,128,16,64]{3,2,1,0:T(8,128)} %get-tuple-element.9, ...), kind=kLoop, calls=%fused_computation.54 | loop fusion | flops 16777216 | bytes 25690112 | tf_op jit(solution)/shard_map/convert.2
  85.4 6.2 pad_maximum_fusion.1
  91.6 10.7 %all-to-all-start.2 = ((bf16[8,128,16,128]{3,1,0,2:T(8,128)(2,1)}), bf16[8,128,16,128]{3,1,0,2:T(8,128)(2,1)}, u32[]{:S(2)}, u32[]{:S(2)}) async-start(bf16[8,128,16,128]{3,1,0,2:T(8,128)(2,1)} %pad_maximum_fusion.1), calls=%async_computation.2 | async-start | bytes 8388608 | tf_op jit(solution)/shard_map/all_to_all | solution.py:67
  102.3 6.0 pad_maximum_fusion
  108.3 86.8 %all-to-all-done.2 = bf16[8,128,16,128]{3,1,0,2:T(8,128)(2,1)} async-done(((bf16[8,128,16,128]{3,1,0,2:T(8,128)(2,1)}), bf16[8,128,16,128]{3,1,0,2:T(8,128)(2,1)}, u32[]{:S(2)}, u32[]{:S(2)}) %all-to-all-start.2) | async-done | bytes 4194336 | tf_op jit(solution)/shard_map/all_to_all | solution.py:67
  195.1 9.0 %all-to-all-start.1 = ((bf16[8,128,16,128]{3,1,0,2:T(8,128)(2,1)}), bf16[8,128,16,128]{3,1,0,2:T(8,128)(2,1)}, u32[]{:S(2)}, u32[]{:S(2)}) async-start(bf16[8,128,16,128]{3,1,0,2:T(8,128)(2,1)} %pad_maximum_fusion), calls=%async_computation.1 | async-start | bytes 8388608 | tf_op jit(solution)/shard_map/all_to_all | solution.py:66
  204.1 12.5 %convert_bitcast_fusion = bf16[8,16,16,8,128]{4,3,2,1,0:T(8,128)(2,1)S(1)} fusion(bf16[8,128,2048]{2,1,0:T(8,128)(2,1)} %param.9, bf16[2048,2048]{1,0:T(8,128)(2,1)} %param.13), kind=kOutput, calls=%fused_computation.83 | convolution fusion | flops 8592031744 | bytes 16777216 | tf_op jit(solution)/shard_map/bsd,de->bse/dot_general | solution.py:34
  216.6 3.1 copy.48
  219.7 77.1 %all-to-all-done.1 = bf16[8,128,16,128]{3,1,0,2:T(8,128)(2,1)} async-done(((bf16[8,128,16,128]{3,1,0,2:T(8,128)(2,1)}), bf16[8,128,16,128]{3,1,0,2:T(8,128)(2,1)}, u32[]{:S(2)}, u32[]{:S(2)}) %all-to-all-start.1) | async-done | bytes 4194336 | tf_op jit(solution)/shard_map/all_to_all | solution.py:66
  296.9 9.8 %all-to-all-start = ((bf16[8,128,16,128]{3,1,0,2:T(8,128)(2,1)}), bf16[8,128,16,128]{3,1,0,2:T(8,128)(2,1)}, u32[]{:S(2)}, u32[]{:S(2)}) async-start(bf16[8,128,16,128]{3,1,0,2:T(8,128)(2,1)} %bitcast.259), calls=%async_computation | async-start | bytes 8388608 | tf_op jit(solution)/shard_map/all_to_all | solution.py:68
  307.1 0.9 iota_compare_fusion.4
  308.1 0.2 iota_compare_fusion.3
  308.3 1.1 iota_compare_fusion.2
  309.4 0.3 iota_compare_fusion.1
  309.7 1.2 iota_compare_fusion
  310.9 2.5 copy.24
  313.4 4.0 copy.21
  317.5 3.1 fusion.99
  320.5 3.6 fusion.75
  324.1 4.6 fusion.69
  328.7 6.4 fusion.63
  335.0 7.3 %fusion.61 = f32[8,256,1792]{2,1,0:T(8,128)} fusion(bf16[8,2048,1,128]{3,1,0,2:T(8,128)(2,1)S(1)} %bitcast.251, bf16[8,2048,1,128]{3,1,0,2:T(8,128)(2,1)S(1)} %bitcast.265), kind=kOutput, calls=%fused_computation.90 | convolution fusion | flops 939524096 | bytes 18874368 | tf_op jit(solution)/shard_map/bqhd,bkhd->bhqk/dot_general | solution.py:51
  342.3 56.8 %all-to-all-done = bf16[8,128,16,128]{3,1,0,2:T(8,128)(2,1)} async-done(((bf16[8,128,16,128]{3,1,0,2:T(8,128)(2,1)}), bf16[8,128,16,128]{3,1,0,2:T(8,128)(2,1)}, u32[]{:S(2)}, u32[]{:S(2)}) %all-to-all-start) | async-done | bytes 4194336 | tf_op jit(solution)/shard_map/all_to_all | solution.py:68
  399.1 6.8 copy.18
  405.9 7.3 %all_to_all.53 = bf16[8,2048,1,128]{1,3,0,2:T(8,128)(2,1)} reshape(bf16[8,16,128,1,128]{2,1,4,0,3:T(8,128)(2,1)} %copy.18) | data formatting | bytes 8388608 | tf_op jit(solution)/shard_map/all_to_all | solution.py:68
  413.2 7.4 %reshape.344 = bf16[8,2048,128]{1,2,0:T(8,128)(2,1)} reshape(bf16[8,16,128,1,128]{2,1,4,0,3:T(8,128)(2,1)} %copy.18) | data formatting | bytes 8388608 | tf_op jit(solution)/shard_map/reshape.65
  420.7 3.3 fusion.123
  424.0 10.2 %fusion.127 = (f32[8,256]{1,0:T(8,128)}, f32[8,256,1280]{2,1,0:T(8,128)}) fusion(pred[256,1280]{1,0:T(8,128)(4,1)S(1)} %iota_compare_fusion.3, bf16[8,2048,1,128]{3,1,0,2:T(8,128)(2,1)} %bitcast.253, bf16[8,2048,1,128]{3,1,0,2:T(8,128)(2,1)} %bitcast.267), kind=kOutput, calls=%fused_computation.202 | convolution fusion | flops 681575680 | bytes 13967360 | tf_op jit(solution)/shard_map/sub | solution.py:54
  434.2 10.6 %fusion.103 = f32[8,256,2048]{2,1,0:T(8,128)} fusion(bf16[8,2048,128]{2,1,0:T(8,128)(2,1)} %bitcast.254, bf16[8,2048,1,128]{3,1,0,2:T(8,128)(2,1)} %bitcast.268), kind=kOutput, calls=%fused_computation.156 | convolution fusion | flops 1073741824 | bytes 21495808 | tf_op jit(solution)/shard_map/bqhd,bkhd->bhqk/dot_general | solution.py:51
  444.7 3.8 fusion.124
  448.5 10.2 %fusion.125 = (f32[8,256]{1,0:T(8,128)S(1)}, f32[8,256,768]{2,1,0:T(8,128)}) fusion(f32[8,256,768]{2,1,0:T(8,128)} %fusion.75, pred[256,768]{1,0:T(8,128)(4,1)S(1)} %iota_compare_fusion.5), kind=kOutput, calls=%fused_computation.200 | output fusion | flops 9437951 | bytes 12787712 | tf_op jit(solution)/shard_map/sub | solution.py:54
  458.8 13.2 %fusion.126 = (f32[8,256]{1,0:T(8,128)S(1)}, f32[8,256,1024]{2,1,0:T(8,128)}) fusion(f32[8,256,1024]{2,1,0:T(8,128)} %fusion.69, pred[256,1024]{1,0:T(8,128)(4,1)S(1)} %copy-done.8), kind=kOutput, calls=%fused_computation.201 | output fusion | flops 12583935 | bytes 17047552 | tf_op jit(solution)/shard_map/sub | solution.py:54
  471.9 10.1 %fusion.128 = (f32[8,256]{1,0:T(8,128)}, f32[8,256,1536]{2,1,0:T(8,128)}) fusion(f32[8,256,1536]{2,1,0:T(8,128)S(1)} %bitcast.270, pred[256,1536]{1,0:T(8,128)(4,1)} %iota_compare_fusion.2), kind=kOutput, calls=%fused_computation.203 | output fusion | flops 18875904 | bytes 25567232 | tf_op jit(solution)/shard_map/sub | solution.py:54
  482.1 18.8 %fusion.129 = (f32[8,256]{1,0:T(8,128)S(1)}, f32[8,256,1792]{2,1,0:T(8,128)}) fusion(f32[8,256,1792]{2,1,0:T(8,128)} %fusion.61, pred[256,1792]{1,0:T(8,128)(4,1)S(1)} %iota_compare_fusion.1), kind=kOutput, calls=%fused_computation.204 | output fusion | flops 22021888 | bytes 29827072 | tf_op jit(solution)/shard_map/sub | solution.py:54
  500.9 21.1 %fusion.130 = (f32[8,256]{1,0:T(8,128)S(1)}, f32[8,256,2048]{2,1,0:T(8,128)}) fusion(f32[8,256,2048]{2,1,0:T(8,128)} %fusion.103, pred[256,2048]{1,0:T(8,128)(4,1)S(1)} %copy-done.7), kind=kOutput, calls=%fused_computation.205 | output fusion | flops 25167872 | bytes 34086912 | tf_op jit(solution)/shard_map/sub | solution.py:54
  522.0 1.5 fusion.88
  523.5 0.8 copy-done.4
  524.3 1.3 copy-done.12
  525.6 1.0 fusion.86
  526.8 0.8 slice-done.4
  527.6 1.3 fusion.98
  528.9 1.1 slice-done.6
  530.1 2.1 fusion.84
  532.2 6.0 fusion.96
  538.2 7.0 fusion.94
  545.3 2.0 copy-done.6
  547.3 8.9 %fusion.92 = bf16[8,2048,1,128]{1,3,0,2:T(8,128)(2,1)} fusion(bf16[8,2048,1,128]{1,3,0,2:T(8,128)(2,1)} %copy-done.6, f32[8,256,1792]{2,1,0:T(8,128)} %get-tuple-element.34, f32[8,256]{1,0:T(8,128)S(1)} %get-tuple-element.33, bf16[8,2048,1,128]{1,3,0,2:T(8,128)(2,1)S(1)} %copy-done.4), kind=kOutput, calls=%fused_computation.138 | convolution fusion | flops 947126272 | bytes 18882560 | tf_op jit(solution)/shard_map/bhqk,bkhd->bqhd/dot_general | solution.py:55
  556.2 9.7 %fusion.90 = bf16[8,2048,1,128]{1,3,0,2:T(8,128)(2,1)} fusion(bf16[8,2048,1,128]{1,3,0,2:T(8,128)(2,1)} %fusion.92, bf16[8,2048,128]{1,2,0:T(8,128)(2,1)S(1)} %copy-done.3, f32[8,256,2048]{2,1,0:T(8,128)} %get-tuple-element.36, f32[8,256]{1,0:T(8,128)S(1)} %get-tuple-element.35), kind=kOutput, calls=%fused_computation.136 | convolution fusion | flops 1082392576 | bytes 21504000 | tf_op jit(solution)/shard_map/bhqk,bkhd->bqhd/dot_general | solution.py:55
  565.9 6.8 copy.28
  572.7 9.8 %all-to-all-start.3 = ((bf16[8,2048,1,128]{3,0,2,1:T(8,128)(2,1)}), bf16[8,2048,1,128]{3,0,2,1:T(8,128)(2,1)}, u32[]{:S(2)}, u32[]{:S(2)}) async-start(bf16[8,2048,1,128]{3,0,2,1:T(8,128)(2,1)} %copy.28), calls=%async_computation.3 | async-start | bytes 8388608 | tf_op jit(solution)/shard_map/all_to_all | solution.py:70
  582.5 92.4 %all-to-all-done.3 = bf16[8,2048,1,128]{3,0,2,1:T(8,128)(2,1)} async-done(((bf16[8,2048,1,128]{3,0,2,1:T(8,128)(2,1)}), bf16[8,2048,1,128]{3,0,2,1:T(8,128)(2,1)}, u32[]{:S(2)}, u32[]{:S(2)}) %all-to-all-start.3) | async-done | bytes 4194336 | tf_op jit(solution)/shard_map/all_to_all | solution.py:70
  674.9 6.9 copy.49
  681.8 7.3 %reshape.347 = bf16[8,128,2048]{2,1,0:T(8,128)(2,1)} reshape(bf16[8,128,16,1,128]{4,2,1,0,3:T(8,128)(2,1)} %bitcast.260) | data formatting | bytes 8388608 | tf_op jit(solution)/shard_map/reshape | solution.py:70
  689.1 12.8 %fusion.16 = (f32[8,128]{1,0:T(8,128)S(1)}, bf16[8,128,2048]{2,1,0:T(8,128)(2,1)S(1)}) fusion(bf16[8,128,2048]{2,1,0:T(8,128)(2,1)} %reshape.347, bf16[2048,2048]{1,0:T(8,128)(2,1)} %param.14), kind=kOutput, calls=%fused_computation.34 | convolution fusion | flops 8598322176 | bytes 16781312 | tf_op jit(solution)/shard_map/bsd,de->bse/dot_general | solution.py:34
  701.9 3.8 fusion.19
  (61 shorter events, 0.7 us)
Async XLA Ops:
  16.2 13.2 %copy-start.9 = (bf16[2048]{0:T(1024)(128)(2,1)S(1)}, bf16[2048]{0:T(1024)(128)(2,1)}, u32[]{:S(2)}) copy-start(bf16[2048]{0:T(1024)(128)(2,1)} %param.16) | copy-start | bytes 12292
  30.3 5.2 copy-start.11
  91.6 103.5 %all-to-all-start.2 = ((bf16[8,128,16,128]{3,1,0,2:T(8,128)(2,1)}), bf16[8,128,16,128]{3,1,0,2:T(8,128)(2,1)}, u32[]{:S(2)}, u32[]{:S(2)}) async-start(bf16[8,128,16,128]{3,1,0,2:T(8,128)(2,1)} %pad_maximum_fusion.1), calls=%async_computation.2 | async-start | bytes 8388608 | tf_op jit(solution)/shard_map/all_to_all | solution.py:67
  195.1 101.8 %all-to-all-start.1 = ((bf16[8,128,16,128]{3,1,0,2:T(8,128)(2,1)}), bf16[8,128,16,128]{3,1,0,2:T(8,128)(2,1)}, u32[]{:S(2)}, u32[]{:S(2)}) async-start(bf16[8,128,16,128]{3,1,0,2:T(8,128)(2,1)} %pad_maximum_fusion), calls=%async_computation.1 | async-start | bytes 8388608 | tf_op jit(solution)/shard_map/all_to_all | solution.py:66
  296.9 102.2 %all-to-all-start = ((bf16[8,128,16,128]{3,1,0,2:T(8,128)(2,1)}), bf16[8,128,16,128]{3,1,0,2:T(8,128)(2,1)}, u32[]{:S(2)}, u32[]{:S(2)}) async-start(bf16[8,128,16,128]{3,1,0,2:T(8,128)(2,1)} %bitcast.259), calls=%async_computation | async-start | bytes 8388608 | tf_op jit(solution)/shard_map/all_to_all | solution.py:68
  313.4 21.6 %copy-start = (bf16[8,16,128,1,128]{4,2,1,0,3:T(8,128)(2,1)}, bf16[8,16,128,1,128]{4,2,1,0,3:T(8,128)(2,1)S(1)}, u32[]{:S(2)}) copy-start(bf16[8,16,128,1,128]{4,2,1,0,3:T(8,128)(2,1)S(1)} %copy.24) | copy-start | bytes 12582916
  317.5 17.6 %copy-start.1 = (bf16[8,16,128,1,128]{4,2,1,0,3:T(8,128)(2,1)}, bf16[8,16,128,1,128]{4,2,1,0,3:T(8,128)(2,1)S(1)}, u32[]{:S(2)}) copy-start(bf16[8,16,128,1,128]{4,2,1,0,3:T(8,128)(2,1)S(1)} %copy.21) | copy-start | bytes 12582916
  434.2 10.6 %copy-start.5 = (f32[8,256,512]{2,1,0:T(8,128)S(1)}, f32[8,256,512]{2,1,0:T(8,128)}, u32[]{:S(2)}) copy-start(f32[8,256,512]{2,1,0:T(8,128)} %fusion.99) | copy-start | bytes 12582916
  448.5 10.2 %copy-start.8 = (pred[256,1024]{1,0:T(8,128)(4,1)S(1)}, pred[256,1024]{1,0:T(8,128)(4,1)}, u32[]{:S(2)}) copy-start(pred[256,1024]{1,0:T(8,128)(4,1)} %iota_compare_fusion.4) | copy-start | bytes 786436
  448.5 23.4 %slice-start = ((s8[12582912]{0:T(1024)(128)(4,1)}), s8[4194304]{0:T(1024)(128)(4,1)S(1)}, s32[]{:S(2)}) async-start(s8[12582912]{0:T(1024)(128)(4,1)} %bitcast.269), calls=%async_computation.4 | async-start | bytes 8388608
  448.5 23.4 %slice-start.1 = ((s8[12582912]{0:T(1024)(128)(4,1)}), s8[4194304]{0:T(1024)(128)(4,1)S(1)}, s32[]{:S(2)}) async-start(s8[12582912]{0:T(1024)(128)(4,1)} %bitcast.269), calls=%async_computation.5 | async-start | bytes 8388608
  458.7 13.2 %slice-start.2 = ((s8[12582912]{0:T(1024)(128)(4,1)}), s8[4194304]{0:T(1024)(128)(4,1)S(1)}, s32[]{:S(2)}) async-start(s8[12582912]{0:T(1024)(128)(4,1)} %bitcast.269), calls=%async_computation.6 | async-start | bytes 8388608
  482.1 18.8 %copy-start.7 = (pred[256,2048]{1,0:T(8,128)(4,1)S(1)}, pred[256,2048]{1,0:T(8,128)(4,1)}, u32[]{:S(2)}) copy-start(pred[256,2048]{1,0:T(8,128)(4,1)} %iota_compare_fusion) | copy-start | bytes 1572868
  500.9 21.1 %copy-start.13 = (f32[8,256,256]{1,2,0:T(8,128)S(1)}, f32[8,256,256]{1,2,0:T(8,128)}, u32[]{:S(2)}) copy-start(f32[8,256,256]{1,2,0:T(8,128)} %get-tuple-element.22) | copy-start | bytes 6291460
  522.0 2.4 copy-start.4
  522.0 3.6 copy-start.12
  522.0 4.8 slice-start.3
  525.6 2.0 slice-start.4
  525.6 3.3 slice-start.5
  527.6 2.4 slice-start.6
  530.1 2.1 copy-start.15
  532.2 6.0 copy-start.14
  545.3 2.0 copy-start.6
  547.3 8.9 %copy-start.3 = (bf16[8,2048,128]{1,2,0:T(8,128)(2,1)S(1)}, bf16[8,2048,128]{1,2,0:T(8,128)(2,1)}, u32[]{:S(2)}) copy-start(bf16[8,2048,128]{1,2,0:T(8,128)(2,1)} %reshape.344) | copy-start | bytes 12582916
  572.7 9.8 %copy-start.10 = (bf16[2048]{0:T(1024)(128)(2,1)S(1)}, bf16[2048]{0:T(1024)(128)(2,1)}, u32[]{:S(2)}) copy-start(bf16[2048]{0:T(1024)(128)(2,1)} %param.17) | copy-start | bytes 12292
  572.7 102.2 %all-to-all-start.3 = ((bf16[8,2048,1,128]{3,0,2,1:T(8,128)(2,1)}), bf16[8,2048,1,128]{3,0,2,1:T(8,128)(2,1)}, u32[]{:S(2)}, u32[]{:S(2)}) async-start(bf16[8,2048,1,128]{3,0,2,1:T(8,128)(2,1)} %copy.28), calls=%async_computation.3 | async-start | bytes 8388608 | tf_op jit(solution)/shard_map/all_to_all | solution.py:70
  689.1 12.8 %copy-start.2 = (bf16[8,128,2048]{2,1,0:T(8,128)(2,1)S(1)}, bf16[8,128,2048]{2,1,0:T(8,128)(2,1)}, u32[]{:S(2)}) copy-start(bf16[8,128,2048]{2,1,0:T(8,128)(2,1)} %param.9) | copy-start | bytes 12582916
where the time goes:
time: 714 us; the launch traced here: 706 us
  waiting for transfers between devices  313 us (44%)
  matrix products  137 us (19%)
  other arithmetic  133 us (19%)
  local copies, waits for them, and re-layouts  82.7 us (12%)
  starting transfers between devices  39.3 us (6%)
    all_to_all x1, waiting for transfers between devices, local_block(): lax.all_to_all(o_heads, 'sp', 1, 2, tiled=True)  92.4 us
    all_to_all x1, waiting for transfers between devices, local_block(): k_heads = lax.all_to_all(k_loc, 'sp', 2, 1, tiled=True)  86.8 us
    sub x6, other arithmetic, causal_attention(): probs = jax.nn.softmax(scores, axis=-1).astype(jnp.bfloat16)  77.2 us
    all_to_all x1, waiting for transfers between devices, local_block(): q_heads = lax.all_to_all(q_loc, 'sp', 2, 1, tiled=True)  77.1 us
    all_to_all x1, waiting for transfers between devices, local_block(): v_heads = lax.all_to_all(v_loc, 'sp', 2, 1, tiled=True)  56.8 us
    dot_general x4, matrix products, project(): jnp.einsum('bsd,de->bse', x_tok, weight, preferred_element_type=jnp.float32)  51 us
    dot_general x8, matrix products, causal_attention(): jnp.einsum('bhqk,bkhd->bqhd', probs, v_heads[:, :key_end], preferred_elem...  37.5 us
    dot_general x6, matrix products, causal_attention(): jnp.einsum('bqhd,bkhd->bhqk', q_blk, k_heads[:, :key_end], preferred_elem...  35.4 us
  transfers between devices with their start and end apart: 4, of which 4 were waited for; matrix products, arithmetic and copies ran while one was open for 8% of the time, Pallas kernels for 0%

commit v1 on v0

v1 whole, which is shorter than its diff:
```python
import functools

import jax
import jax.numpy as jnp
import numpy as np
from jax import lax
from jax.experimental import pallas as pl
from jax.experimental.pallas import tpu as pltpu
from jax.sharding import PartitionSpec as P

HEAD_DIM = 128
ROPE_THETA = 500000.0
NORM_EPS = 1e-6
SCALE = HEAD_DIM ** -0.5
LOG2E = 1.4426950408889634
MESH = pl.DeviceIdType.MESH
BF = jnp.bfloat16
F32 = jnp.float32
CORES = 2
NT = 512
HG = 4


def lane_fold(vals):
    total = vals[:, :HEAD_DIM]
    for start in range(HEAD_DIM, vals.shape[1], HEAD_DIM):
        total = total + vals[:, start:start + HEAD_DIM]
    return total


def block_kernel(n_z, x_ref, pos_ref, wq_ref, wk_ref, wv_ref, wo_ref, freq_ref, gq_ref, gk_ref, ga_ref, y_ref,
                 wbuf, xbuf, pbuf, qbuf, kbuf, vbuf, raw, obuf, sscr, acc, lsum, tabs,
                 wsem, xsend, xrecv, psend, precv, ksend, krecv, vsend, vrecv, ysend, yrecv):
    seq_loc, width = xbuf.shape[1], xbuf.shape[2]
    heads = width // HEAD_DIM
    me = lax.axis_index('sp')
    dp = lax.axis_index('dp')
    z = me // CORES
    c = me % CORES
    other = z * CORES + (1 - c)

    def peer(zz):
        return (dp, zz * CORES + c)

    def src_z(t):
        half = (t + 1) // 2
        sign = 1 - 2 * ((t + 1) % 2)
        return (z + half * sign + n_z) % n_z

    def w_copy(i, ref):
        return pltpu.make_async_copy(ref, wbuf.at[i], wsem.at[i])

    w_copies = [w_copy(0, wk_ref), w_copy(1, wv_ref), w_copy(2, wq_ref), w_copy(3, wo_ref)]

    def x_copy(zz, slot):
        return pltpu.make_async_remote_copy(src_ref=x_ref.at[zz], dst_ref=xbuf.at[slot], send_sem=xsend.at[zz],
                                            recv_sem=xrecv.at[slot], device_id=peer(zz), device_id_type=MESH)

    def p_copy(zz, slot):
        return pltpu.make_async_remote_copy(src_ref=pos_ref.at[zz], dst_ref=pbuf.at[slot], send_sem=psend.at[zz],
                                            recv_sem=precv.at[slot], device_id=peer(zz), device_id_type=MESH)

    def kv_copy(buf, ssem, rsem, zz, core):
        return pltpu.make_async_remote_copy(src_ref=buf.at[zz, core], dst_ref=buf.at[zz, core], send_sem=ssem.at[zz],
                                            recv_sem=rsem.at[zz], device_id=(dp, other), device_id_type=MESH)

    def y_copy(zz, slot):
        return pltpu.make_async_remote_copy(src_ref=xbuf.at[zz], dst_ref=y_ref.at[slot], send_sem=ysend.at[zz],
                                            recv_sem=yrecv.at[slot], device_id=peer(zz), device_id_type=MESH)

    own_x = pltpu.make_async_copy(x_ref.at[z], xbuf.at[z], xrecv.at[z])
    own_p = pltpu.make_async_copy(pos_ref.at[z], pbuf.at[z], precv.at[z])
    own_x.start()
    own_p.start()

    barrier = pltpu.get_barrier_semaphore()
    for d in range(1, n_z):
        pl.semaphore_signal(barrier, inc=1, device_id=peer((z + d) % n_z), device_id_type=MESH)
    pl.semaphore_signal(barrier, inc=1, device_id=(dp, other), device_id_type=MESH)
    pl.semaphore_wait(barrier, n_z)

    for t in range(1, n_z):
        p_copy(src_z(t), z).start()
        x_copy(src_z(t), z).start()
    for cp in w_copies:
        cp.start()

    def matmul_stats(src, wi):
        def tile(n, ss):
            cols = pl.ds(pl.multiple_of(n * NT, NT), NT)
            prod = jnp.dot(src[...], wbuf[wi, :, cols], preferred_element_type=F32).astype(BF)
            raw[:, cols] = prod
            wide = prod.astype(F32)
            return ss + lane_fold(wide * wide)
        ss = lax.fori_loop(0, width // NT, tile, jnp.zeros((seq_loc, HEAD_DIM), F32))
        return lax.rsqrt(jnp.sum(ss, axis=-1, keepdims=True) * (1.0 / width) + NORM_EPS)

    def norm_rope(scale, gain_ref, dst):
        def quad(h4, carry):
            for i in range(4):
                cols = pl.ds(pl.multiple_of((h4 * 4 + i) * HEAD_DIM, HEAD_DIM), HEAD_DIM)
                u = raw[:, cols].astype(F32) * scale * gain_ref[:, cols]
                dst[:, cols] = (u * tabs[0] + pltpu.roll(u, HEAD_DIM // 2, 1) * tabs[1]).astype(BF)
            return carry
        lax.fori_loop(0, heads // 4, quad, 0)

    def make_tables(zz):
        row = jnp.broadcast_to(pbuf[zz].astype(F32), (seq_loc, seq_loc))
        angle = jnp.transpose(row) * freq_ref[...]
        lane = lax.broadcasted_iota(jnp.int32, (seq_loc, HEAD_DIM), 1)
        sin_t = jnp.sin(angle)
        tabs[0] = jnp.cos(angle)
        tabs[1] = jnp.where(lane < HEAD_DIM // 2, -sin_t, sin_t)

    def qkv_block(zz):
        make_tables(zz)
        src = xbuf.at[zz]
        norm_rope(matmul_stats(src, 0), gk_ref, kbuf.at[zz, c])

        def v_tile(n, carry):
            cols = pl.ds(pl.multiple_of(n * NT, NT), NT)
            vbuf[zz, c, :, cols] = jnp.dot(src[...], wbuf[1, :, cols], preferred_element_type=F32).astype(BF)
            return carry
        lax.fori_loop(0, width // NT, v_tile, 0)
        kv_copy(kbuf, ksend, krecv, zz, c).start()
        norm_rope(matmul_stats(src, 2), gq_ref, qbuf.at[zz])
        kv_copy(vbuf, vsend, vrecv, zz, c).start()

    own_x.wait()
    own_p.wait()
    for cp in w_copies[:3]:
        cp.wait()
    qkv_block(z)

    def phase1(t, carry):
        zz = src_z(t)
        p_copy(z, zz).wait_recv()
        x_copy(z, zz).wait_recv()
        qkv_block(zz)
        return carry
    lax.fori_loop(1, n_z, phase1, 0)

    w_copies[3].wait()

    def kv_wait(zz, carry):
        kv_copy(kbuf, ksend, krecv, zz, 1 - c).wait_recv()
        kv_copy(vbuf, vsend, vrecv, zz, 1 - c).wait_recv()
        return carry
    lax.fori_loop(0, n_z, kv_wait, 0)

    keys = CORES * seq_loc
    lim = SCALE * LOG2E

    def attend(zz):
        def group(g, carry):
            def cols_of(i):
                return pl.ds(pl.multiple_of((g * HG + i) * HEAD_DIM, HEAD_DIM), HEAD_DIM)

            def score(i, kz):
                k = kbuf[kz, :, :, cols_of(i)].reshape(keys, HEAD_DIM)
                return lax.dot_general(qbuf[zz, :, cols_of(i)], k, (((1,), (1,)), ((), ())), preferred_element_type=F32)

            row = lax.broadcasted_iota(jnp.int32, (seq_loc, keys), 0) + c * seq_loc
            col = lax.broadcasted_iota(jnp.int32, (seq_loc, keys), 1)
            tops = []
            for i in range(HG):
                s = jnp.where(col <= row, score(i, zz), -1e30)
                sscr[i, zz] = s
                tops.append(jnp.maximum(s[:, :seq_loc], s[:, seq_loc:]))

            def body_a(kz, tops):
                new = []
                for i in range(HG):
                    s = score(i, kz)
                    sscr[i, kz] = s
                    new.append(jnp.maximum(tops[i], jnp.maximum(s[:, :seq_loc], s[:, seq_loc:])))
                return tuple(new)
            tops = lax.fori_loop(0, zz, body_a, tuple(tops))
            peak = [jnp.max(t, axis=-1, keepdims=True) for t in tops]
            for i in range(HG):
                acc[i] = jnp.zeros((seq_loc, HEAD_DIM), F32)
                lsum[i] = jnp.zeros((seq_loc, HEAD_DIM), F32)

            def body_b(kz, carry):
                for i in range(HG):
                    p = jnp.exp2((sscr[i, kz] - peak[i]) * lim)
                    lsum[i] += p[:, :seq_loc] + p[:, seq_loc:]
                    v = vbuf[kz, :, :, cols_of(i)].reshape(keys, HEAD_DIM)
                    acc[i] += jnp.dot(p.astype(BF), v, preferred_element_type=F32)
                return carry
            lax.fori_loop(0, zz + 1, body_b, 0)
            for i in range(HG):
                total = jnp.sum(lsum[i], axis=-1, keepdims=True)
                obuf[:, cols_of(i)] = (acc[i] / total).astype(BF)
            return carry
        lax.fori_loop(0, heads // HG, group, 0)

    def out_block(zz):
        scale = matmul_stats(obuf, 3)

        def tile(n, carry):
            cols = pl.ds(pl.multiple_of(n * NT, NT), NT)
            y = xbuf[zz, :, cols].astype(F32) + raw[:, cols].astype(F32) * scale * ga_ref[:, cols]
            xbuf[zz, :, cols] = y.astype(BF)
            return carry
        lax.fori_loop(0, width // NT, tile, 0)

    def phase2(u, carry):
        zz = src_z(n_z - 1 - u)
        attend(zz)
        out_block(zz)
        y_copy(zz, z).start()
        return carry
    lax.fori_loop(0, n_z - 1, phase2, 0)
    attend(z)
    out_block(z)
    own_y = pltpu.make_async_copy(xbuf.at[z], y_ref.at[z], yrecv.at[z])
    own_y.start()

    def drain(t, carry):
        zz = src_z(t)
        p_copy(zz, z).wait_send()
        x_copy(zz, z).wait_send()
        y_copy(zz, z).wait_send()
        y_copy(z, zz).wait_recv()
        return carry
    lax.fori_loop(1, n_z, drain, 0)

    def kv_drain(zz, carry):
        kv_copy(kbuf, ksend, krecv, zz, c).wait_send()
        kv_copy(vbuf, vsend, vrecv, zz, c).wait_send()
        return carry
    lax.fori_loop(0, n_z, kv_drain, 0)
    own_y.wait()


def solution(mesh):
    n_z = mesh.shape['sp'] // CORES

    def local_block(x_loc, pos_loc, w_query, w_key, w_value, w_out, gain_q, gain_k, gain_out):
        batch, seq_loc, width = x_loc.shape
        inv_freq = 1.0 / (ROPE_THETA ** (np.arange(0, HEAD_DIM, 2, dtype=np.float32) / HEAD_DIM))
        freq = jnp.asarray(np.concatenate([inv_freq, inv_freq]).astype(np.float32)[None, :])
        any_spec = pl.BlockSpec(memory_space=pl.ANY)
        vmem = pl.BlockSpec(memory_space=pltpu.VMEM)
        dma = pltpu.SemaphoreType.DMA
        f32_gain = [g.astype(F32)[None, :] for g in (gain_q, gain_k, gain_out)]
        return pl.pallas_call(
            functools.partial(block_kernel, n_z),
            out_shape=jax.ShapeDtypeStruct(x_loc.shape, BF),
            in_specs=[any_spec] * 6 + [vmem] * 4,
            out_specs=any_spec,
            scratch_shapes=[
                pltpu.VMEM((4, width, width), BF),
                pltpu.VMEM((n_z, seq_loc, width), BF),
                pltpu.VMEM((n_z, 1, seq_loc), jnp.int32),
                pltpu.VMEM((n_z, seq_loc, width), BF),
                pltpu.VMEM((n_z, CORES, seq_loc, width), BF),
                pltpu.VMEM((n_z, CORES, seq_loc, width), BF),
                pltpu.VMEM((seq_loc, width), BF),
                pltpu.VMEM((seq_loc, width), BF),
                pltpu.VMEM((HG, n_z, seq_loc, CORES * seq_loc), F32),
                pltpu.VMEM((HG, seq_loc, HEAD_DIM), F32),
                pltpu.VMEM((HG, seq_loc, HEAD_DIM), F32),
                pltpu.VMEM((2, seq_loc, HEAD_DIM), F32),
                dma((4,)),
            ] + [dma((n_z,))] * 10,
            compiler_params=pltpu.CompilerParams(collective_id=0, has_side_effects=True, vmem_limit_bytes=67043328),
        )(x_loc, pos_loc[:, None, :], w_query, w_key, w_value, w_out, freq, *f32_gain)

    tok_spec = P('dp', 'sp', None)
    return jax.shard_map(local_block, mesh=mesh, in_specs=(tok_spec, P('dp', 'sp'), P(), P(), P(), P(), P(), P(), P()), out_specs=tok_spec, check_vma=False)
```

time: 714 us -> 242 us (0.34)
  waiting for transfers between devices: 313 us -> 0 us
  Pallas kernels: 0 us -> 232 us
  matrix products: 137 us -> 0 us
  other arithmetic: 133 us -> 3.85 us
  local copies, waits for them, and re-layouts: 82.7 us -> 4.79 us
  starting transfers between devices: 39.3 us -> 0 us
    all_to_all x4 -> x0, waiting for transfers between devices: 313 us -> none  [the longest x1 92.4 us: local_block(): lax.all_to_all(o_heads, 'sp', 1, 2, tiled=True)]
    pallas_call x0 -> x1, Pallas kernels: none -> 232 us  [local_block(): pl.pallas_call(functools.partial(block_kernel, n_z), out_shape=jax.ShapeD...]
    dot_general x18 -> x0, matrix products: 124 us -> none  [the longest x4 51 us: project(): jnp.einsum('bsd,de->bse', x_tok, weight, preferred_element_type=jnp.float32)]
    sub x6 -> x0, other arithmetic: 77.2 us -> none  [causal_attention(): probs = jax.nn.softmax(scores, axis=-1).astype(jnp.bfloat16)]
    all_to_all x4 -> x0, starting transfers between devices: 39.3 us -> none  [the longest x1 10.7 us: local_block(): k_heads = lax.all_to_all(k_loc, 'sp', 2, 1, tiled=True)]
    another operation x1 -> x0, other arithmetic: 30.9 us -> none
    all_to_all x5 -> x0, local copies, waits for them, and re-layouts: 27.5 us -> none  [the longest x2 14.1 us: local_block(): v_heads = lax.all_to_all(v_loc, 'sp', 2, 1, tiled=True)]
    slice x1 -> x0, local copies, waits for them, and re-layouts: 17 us -> none  [apply_rope(): first = heads_f32[..., :half]]
  transfers between devices with their start and end apart: 4 -> 0, of which waited for: 4 -> 0; matrix products, arithmetic and copies ran while one was open for 8% -> 0% of each run, Pallas kernels for 0% -> 0%
where the time goes in v1:
time: 242 us; the launch traced here: 241 us
  Pallas kernels  232 us (96%)
  local copies, waits for them, and re-layouts  4.79 us (2%)
  other arithmetic  3.85 us (2%)
    pallas_call x1, Pallas kernels, local_block(): pl.pallas_call(functools.partial(block_kernel, n_z), out_shape=jax.ShapeD...  232 us

profile of v1, /device:TPU:21, one launch (start us, length us, event | category | flops | bytes accessed | tf_op | source)
XLA Modules:
  0.0 240.9 jit_solution(15991773129712340643)
XLA Ops:
  0.0 1.3 broadcast_in_dim.25
  1.3 1.3 broadcast_in_dim.26
  2.6 1.3 broadcast_in_dim.27
  3.8 232.2 %shard_map.100 = bf16[8,128,2048]{2,1,0:T(8,128)(2,1)} custom-call(bf16[8,128,2048]{2,1,0:T(8,128)(2,1)} %x_ref.1, s32[8,1,128]{2,1,0:T(1,128)} %bitcast.7, bf16[2048,2048]{1,0:T(8,128)(2,1)} %wq_ref.1, bf16[2048,2048]{1,0:T(8,128)(2,1)} %wk_ref.1, bf16[2048,2048]{1,0:T(8,128)(2,1)} %wv_ref.1, bf16[2048,2048]{1,0:T(8,128)(2,1)} %wo_ref.1, ...), custom_call_target="tpu_custom_call" | custom-call | tf_op jit(solution)/shard_map/pallas_call | solution.py:248
  236.1 4.8 %copy.12 = bf16[8,128,2048]{2,1,0:T(8,128)(2,1)} copy(bf16[8,128,2048]{2,1,0:T(8,128)(2,1)} %shard_map.100) | data formatting | bytes 8388608

commit v2 on v1

v2 whole, which is shorter than its diff:
```python
import functools

import jax
import jax.numpy as jnp
import numpy as np
from jax import lax
from jax.experimental import pallas as pl
from jax.experimental.pallas import tpu as pltpu
from jax.sharding import PartitionSpec as P

HEAD_DIM = 128
ROPE_THETA = 500000.0
NORM_EPS = 1e-6
SCALE = HEAD_DIM ** -0.5
LOG2E = 1.4426950408889634
MESH = pl.DeviceIdType.MESH
BF = jnp.bfloat16
F32 = jnp.float32
CORES = 2
NT = 1024
RG = 8
MAX_HG = 4
SLOTS = 16


def lane_fold(vals):
    total = vals[:, :HEAD_DIM]
    for start in range(HEAD_DIM, vals.shape[1], HEAD_DIM):
        total = total + vals[:, start:start + HEAD_DIM]
    return total


def block_kernel(n_z, x_ref, pos_ref, wq_ref, wk_ref, wv_ref, wo_ref, freq_ref, gq_ref, gk_ref, ga_ref, y_ref,
                 wbuf, xbuf, pbuf, qbuf, kbuf, vbuf, raw, sscr, gains, tabs,
                 wsem, xsend, xrecv, psend, precv, ksend, krecv, vsend, vrecv, ysend, yrecv):
    seq_loc, width = xbuf.shape[1], xbuf.shape[2]
    heads = width // HEAD_DIM
    me = lax.axis_index('sp')
    dp = lax.axis_index('dp')
    z = me // CORES
    c = me % CORES
    other = z * CORES + (1 - c)

    def peer(zz):
        return (dp, zz * CORES + c)

    def src_z(t):
        half = (t + 1) // 2
        sign = 1 - 2 * ((t + 1) % 2)
        return (z + half * sign + n_z) % n_z

    def w_copy(i, ref):
        return pltpu.make_async_copy(ref, wbuf.at[i], wsem.at[i])

    w_copies = [w_copy(0, wk_ref), w_copy(1, wv_ref), w_copy(2, wq_ref), w_copy(3, wo_ref)]

    def x_copy(zz, slot):
        return pltpu.make_async_remote_copy(src_ref=x_ref.at[zz], dst_ref=xbuf.at[slot], send_sem=xsend.at[zz],
                                            recv_sem=xrecv.at[slot], device_id=peer(zz), device_id_type=MESH)

    def p_copy(zz, slot):
        return pltpu.make_async_remote_copy(src_ref=pos_ref.at[zz], dst_ref=pbuf.at[slot], send_sem=psend.at[zz],
                                            recv_sem=precv.at[slot], device_id=peer(zz), device_id_type=MESH)

    def kv_copy(buf, ssem, rsem, zz, core):
        return pltpu.make_async_remote_copy(src_ref=buf.at[zz, core], dst_ref=buf.at[zz, core], send_sem=ssem.at[zz],
                                            recv_sem=rsem.at[zz], device_id=(dp, other), device_id_type=MESH)

    def y_copy(zz, slot):
        return pltpu.make_async_remote_copy(src_ref=xbuf.at[zz], dst_ref=y_ref.at[slot], send_sem=ysend.at[zz],
                                            recv_sem=yrecv.at[slot], device_id=peer(zz), device_id_type=MESH)

    own_x = pltpu.make_async_copy(x_ref.at[z], xbuf.at[z], xrecv.at[z])
    own_p = pltpu.make_async_copy(pos_ref.at[z], pbuf.at[z], precv.at[z])
    own_x.start()
    own_p.start()
    for cp in w_copies:
        cp.start()

    for i, ref in enumerate((gq_ref, gk_ref, ga_ref)):
        for h in range(heads):
            gains[i, h] = ref[h * HEAD_DIM:(h + 1) * HEAD_DIM].astype(F32)[None, :]

    barrier = pltpu.get_barrier_semaphore()
    for d in range(1, n_z):
        pl.semaphore_signal(barrier, inc=1, device_id=peer((z + d) % n_z), device_id_type=MESH)
    pl.semaphore_signal(barrier, inc=1, device_id=(dp, other), device_id_type=MESH)
    pl.semaphore_wait(barrier, n_z)

    for t in range(1, n_z):
        p_copy(src_z(t), z).start()
        x_copy(src_z(t), z).start()

    def matmul_stats(load, wi):
        per = NT // HEAD_DIM

        def tile(n, ss):
            cols = pl.ds(pl.multiple_of(n * NT, NT), NT)
            prod = jnp.dot(load(), wbuf[wi, :, cols], preferred_element_type=F32).astype(BF)
            for i in range(per):
                part = prod[:, i * HEAD_DIM:(i + 1) * HEAD_DIM]
                raw[n * per + i] = part
                wide = part.astype(F32)
                ss = ss + wide * wide
            return ss
        ss = lax.fori_loop(0, width // NT, tile, jnp.zeros((seq_loc, HEAD_DIM), F32))
        return lax.rsqrt(jnp.sum(ss, axis=-1, keepdims=True) * (1.0 / width) + NORM_EPS)

    def norm_rope(scale, gain_ref, dst):
        def some(hg, carry):
            for i in range(RG):
                h = hg * RG + i
                u = raw[h].astype(F32) * scale * gain_ref[h]
                dst[h] = (u * tabs[0] + pltpu.roll(u, HEAD_DIM // 2, 1) * tabs[1]).astype(BF)
            return carry
        lax.fori_loop(0, heads // RG, some, 0)

    def make_tables(zz):
        row = jnp.broadcast_to(pbuf[zz].astype(F32), (seq_loc, seq_loc))
        angle = jnp.transpose(row) * freq_ref[...]
        lane = lax.broadcasted_iota(jnp.int32, (seq_loc, HEAD_DIM), 1)
        sin_t = jnp.sin(angle)
        tabs[0] = jnp.cos(angle)
        tabs[1] = jnp.where(lane < HEAD_DIM // 2, -sin_t, sin_t)

    def qkv_block(zz):
        make_tables(zz)
        src = xbuf.at[zz]
        norm_rope(matmul_stats(lambda: src[...], 0), gains.at[1], kbuf.at[zz, c])

        def v_tile(n, carry):
            cols = pl.ds(pl.multiple_of(n * NT, NT), NT)
            prod = jnp.dot(src[...], wbuf[1, :, cols], preferred_element_type=F32).astype(BF)
            for i in range(NT // HEAD_DIM):
                vbuf[zz, c, n * (NT // HEAD_DIM) + i] = prod[:, i * HEAD_DIM:(i + 1) * HEAD_DIM]
            return carry
        lax.fori_loop(0, width // NT, v_tile, 0)
        kv_copy(kbuf, ksend, krecv, zz, c).start()
        norm_rope(matmul_stats(lambda: src[...], 2), gains.at[0], qbuf.at[zz])
        kv_copy(vbuf, vsend, vrecv, zz, c).start()

    own_x.wait()
    own_p.wait()
    for cp in w_copies[:3]:
        cp.wait()

    def phase1(t, carry):
        zz = src_z(t)

        @pl.when(t > 0)
        def _():
            p_copy(z, zz).wait_recv()
            x_copy(z, zz).wait_recv()
        qkv_block(zz)
        return carry
    lax.fori_loop(0, n_z, phase1, 0)

    w_copies[3].wait()

    def kv_wait(zz, carry):
        kv_copy(kbuf, ksend, krecv, zz, 1 - c).wait_recv()
        kv_copy(vbuf, vsend, vrecv, zz, 1 - c).wait_recv()
        return carry
    lax.fori_loop(0, n_z, kv_wait, 0)

    keys = CORES * seq_loc
    lim = SCALE * LOG2E

    def attend_len(zz, nk):
        hg = MAX_HG if nk * MAX_HG <= SLOTS else 2
        row = lax.broadcasted_iota(jnp.int32, (seq_loc, keys), 0) + c * seq_loc
        col = lax.broadcasted_iota(jnp.int32, (seq_loc, keys), 1)
        seen = col <= row

        def group(g, carry):
            peak = []
            for i in range(hg):
                h = g * hg + i
                q = qbuf[zz, h]
                top = None
                for kz in range(nk):
                    k = kbuf[kz, :, h].reshape(keys, HEAD_DIM)
                    s = lax.dot_general(q, k, (((1,), (1,)), ((), ())), preferred_element_type=F32)
                    if kz == nk - 1:
                        s = jnp.where(seen, s, -1e30)
                    sscr[i * nk + kz] = s
                    fold = jnp.maximum(s[:, :seq_loc], s[:, seq_loc:])
                    top = fold if top is None else jnp.maximum(top, fold)
                peak.append(jnp.max(top, axis=-1, keepdims=True))
            for i in range(hg):
                h = g * hg + i
                total = None
                probs = []
                for kz in range(nk):
                    p = jnp.exp2((sscr[i * nk + kz] - peak[i]) * lim)
                    fold = p[:, :seq_loc] + p[:, seq_loc:]
                    total = fold if total is None else total + fold
                    probs.append(p.astype(BF))
                v = jnp.concatenate([vbuf[kz, :, h].reshape(keys, HEAD_DIM) for kz in range(nk)], axis=0)
                out = jnp.dot(jnp.concatenate(probs, axis=1), v, preferred_element_type=F32)
                denom = jnp.sum(total, axis=-1, keepdims=True)
                qbuf[zz, h] = (out / denom).astype(BF)
            return carry
        lax.fori_loop(0, heads // hg, group, 0)

    def attend(zz):
        for nk in range(1, n_z + 1):
            pl.when(zz == nk - 1)(functools.partial(attend_len, zz, nk))

    def out_block(zz):
        scale = matmul_stats(lambda: jnp.concatenate([qbuf[zz, h] for h in range(heads)], axis=1), 3)

        def some(hg, carry):
            for i in range(RG):
                h = hg * RG + i
                cols = pl.ds(pl.multiple_of(h * HEAD_DIM, HEAD_DIM), HEAD_DIM)
                y = xbuf[zz, :, cols].astype(F32) + raw[h].astype(F32) * scale * gains[2, h]
                xbuf[zz, :, cols] = y.astype(BF)
            return carry
        lax.fori_loop(0, heads // RG, some, 0)

    own_y = pltpu.make_async_copy(xbuf.at[z], y_ref.at[z], yrecv.at[z])

    def phase2(u, carry):
        zz = src_z(n_z - 1 - u)
        attend(zz)
        out_block(zz)

        @pl.when(u < n_z - 1)
        def _():
            y_copy(zz, z).start()
        return carry
    lax.fori_loop(0, n_z, phase2, 0)
    own_y.start()

    def drain(t, carry):
        zz = src_z(t)
        p_copy(zz, z).wait_send()
        x_copy(zz, z).wait_send()
        y_copy(zz, z).wait_send()
        y_copy(z, zz).wait_recv()
        return carry
    lax.fori_loop(1, n_z, drain, 0)

    def kv_drain(zz, carry):
        kv_copy(kbuf, ksend, krecv, zz, c).wait_send()
        kv_copy(vbuf, vsend, vrecv, zz, c).wait_send()
        return carry
    lax.fori_loop(0, n_z, kv_drain, 0)
    own_y.wait()


def solution(mesh):
    n_z = mesh.shape['sp'] // CORES

    def local_block(x_loc, pos_loc, w_query, w_key, w_value, w_out, gain_q, gain_k, gain_out):
        batch, seq_loc, width = x_loc.shape
        inv_freq = 1.0 / (ROPE_THETA ** (np.arange(0, HEAD_DIM, 2, dtype=np.float32) / HEAD_DIM))
        freq = jnp.asarray(np.concatenate([inv_freq, inv_freq]).astype(np.float32)[None, :])
        heads = width // HEAD_DIM
        any_spec = pl.BlockSpec(memory_space=pl.ANY)
        vmem = pl.BlockSpec(memory_space=pltpu.VMEM)
        dma = pltpu.SemaphoreType.DMA
        return pl.pallas_call(
            functools.partial(block_kernel, n_z),
            out_shape=jax.ShapeDtypeStruct(x_loc.shape, BF),
            in_specs=[any_spec] * 6 + [vmem] * 4,
            out_specs=any_spec,
            scratch_shapes=[
                pltpu.VMEM((4, width, width), BF),
                pltpu.VMEM((n_z, seq_loc, width), BF),
                pltpu.VMEM((n_z, 1, seq_loc), jnp.int32),
                pltpu.VMEM((n_z, heads, seq_loc, HEAD_DIM), BF),
                pltpu.VMEM((n_z, CORES, heads, seq_loc, HEAD_DIM), BF),
                pltpu.VMEM((n_z, CORES, heads, seq_loc, HEAD_DIM), BF),
                pltpu.VMEM((heads, seq_loc, HEAD_DIM), BF),
                pltpu.VMEM((SLOTS, seq_loc, CORES * seq_loc), F32),
                pltpu.VMEM((3, heads, 1, HEAD_DIM), F32),
                pltpu.VMEM((2, seq_loc, HEAD_DIM), F32),
                dma((4,)),
            ] + [dma((n_z,))] * 10,
            compiler_params=pltpu.CompilerParams(collective_id=0, has_side_effects=True, vmem_limit_bytes=67043328),
        )(x_loc, pos_loc[:, None, :], w_query, w_key, w_value, w_out, freq, gain_q, gain_k, gain_out)

    tok_spec = P('dp', 'sp', None)
    return jax.shard_map(local_block, mesh=mesh, in_specs=(tok_spec, P('dp', 'sp'), P(), P(), P(), P(), P(), P(), P()), out_specs=tok_spec, check_vma=False)
```

time: 242 us -> 226 us (0.934)
  Pallas kernels: 232 us -> 221 us
  other arithmetic: 3.85 us -> 0 us
    pallas_call x1, Pallas kernels: 232 us -> 221 us  [local_block(): pl.pallas_call(functools.partial(block_kernel, n_z), out_shape=jax.ShapeD...]
    broadcast_in_dim x3 -> x0, other arithmetic: 3.85 us -> none  [local_block(): f32_gain = [g.astype(F32)[None, :] for g in (gain_q, gain_k, gain_out)]]
where the time goes in v2:
time: 226 us
  Pallas kernels  221 us (98%)
  local copies, waits for them, and re-layouts  4.79 us (2%)
    pallas_call x1, Pallas kernels, local_block(): pl.pallas_call(functools.partial(block_kernel, n_z), out_shape=jax.ShapeD...  221 us
    unnamed x1, local copies, waits for them, and re-layouts  4.79 us

profile of v2, /device:TPU:21, one launch (start us, length us, event | category | flops | bytes accessed | tf_op | source)
XLA Modules:
  0.0 226.1 jit_solution(14117926178965880525)
XLA Ops:
  0.0 221.3 %shard_map.100 = bf16[8,128,2048]{2,1,0:T(8,128)(2,1)} custom-call(bf16[8,128,2048]{2,1,0:T(8,128)(2,1)} %x_ref.1, s32[8,1,128]{2,1,0:T(1,128)} %bitcast.1, bf16[2048,2048]{1,0:T(8,128)(2,1)} %wq_ref.1, bf16[2048,2048]{1,0:T(8,128)(2,1)} %wk_ref.1, bf16[2048,2048]{1,0:T(8,128)(2,1)} %wv_ref.1, bf16[2048,2048]{1,0:T(8,128)(2,1)} %wo_ref.1, ...), custom_call_target="tpu_custom_call" | custom-call | tf_op jit(solution)/shard_map/pallas_call | solution.py:264
  221.3 4.8 %copy.12 = bf16[8,128,2048]{2,1,0:T(8,128)(2,1)} copy(bf16[8,128,2048]{2,1,0:T(8,128)(2,1)} %shard_map.100) | data formatting | bytes 8388608

commit v3 on v2

--- a/solution.py
+++ b/solution.py
@@ -21,6 +21,27 @@
 RG = 8
 MAX_HG = 4
 SLOTS = 16
+PER_WORD = 6
+SENDS = [
+    [1, 7, 2, 6, 3, 5, 4],
+    [1, 7, 2, 6, 3, 5, 4],
+    [1, 7, 2, 6, 3, 5, 4],
+    [1, 7, 2, 6, 3, 5, 4],
+    [1, 7, 2, 6, 3, 5, 4],
+    [1, 7, 2, 6, 3, 5, 4],
+    [1, 7, 2, 6, 3, 5, 4],
+    [1, 7, 2, 6, 3, 5, 4],
+]
+STEPS = [
+    [0, 1, 6, 3, 2, 5, 10, 4, 12, 13, 7, 11, 9, 14, 8, 15],
+    [0, 7, 6, 2, 8, 5, 3, 1, 4, 12, 10, 9, 14, 13, 11, 15],
+    [0, 7, 2, 1, 6, 5, 9, 3, 4, 12, 8, 11, 14, 13, 10, 15],
+    [0, 1, 7, 2, 6, 5, 13, 3, 11, 4, 12, 9, 14, 8, 15, 10],
+    [0, 5, 4, 12, 2, 7, 1, 6, 8, 9, 15, 3, 10, 13, 14, 11],
+    [0, 3, 2, 11, 1, 4, 12, 5, 7, 13, 6, 9, 15, 10, 14, 8],
+    [0, 6, 3, 1, 2, 11, 4, 12, 5, 7, 13, 9, 8, 10, 15, 14],
+    [0, 2, 7, 3, 1, 5, 4, 12, 11, 6, 15, 9, 10, 14, 8, 13],
+]
 
 
 def lane_fold(vals):
@@ -44,10 +65,15 @@
     def peer(zz):
         return (dp, zz * CORES + c)
 
-    def src_z(t):
-        half = (t + 1) // 2
-        sign = 1 - 2 * ((t + 1) % 2)
-        return (z + half * sign + n_z) % n_z
+    def code_at(rows, i):
+        val = jnp.int32(0)
+        for start in range(0, len(rows[0]), PER_WORD):
+            words = [sum(v << (4 * j) for j, v in enumerate(row[start:start + PER_WORD])) for row in rows]
+            word = jnp.int32(words[0])
+            for q, w in enumerate(words[1:], 1):
+                word = jnp.where(z == q, w, word)
+            val = jnp.where(i >= start, word, val)
+        return lax.shift_right_logical(val, jnp.int32(4 * (i % PER_WORD))) % 16
 
     def w_copy(i, ref):
         return pltpu.make_async_copy(ref, wbuf.at[i], wsem.at[i])
@@ -87,9 +113,10 @@
     pl.semaphore_signal(barrier, inc=1, device_id=(dp, other), device_id_type=MESH)
     pl.semaphore_wait(barrier, n_z)
 
-    for t in range(1, n_z):
-        p_copy(src_z(t), z).start()
-        x_copy(src_z(t), z).start()
+    for i in range(n_z - 1):
+        zz = (z + code_at(SENDS, i)) % n_z
+        p_copy(zz, z).start()
+        x_copy(zz, z).start()
 
     def matmul_stats(load, wi):
         per = NT // HEAD_DIM
@@ -136,32 +163,15 @@
             return carry
         lax.fori_loop(0, width // NT, v_tile, 0)
         kv_copy(kbuf, ksend, krecv, zz, c).start()
-        norm_rope(matmul_stats(lambda: src[...], 2), gains.at[0], qbuf.at[zz])
+        q_scale = matmul_stats(lambda: src[...], 2)
         kv_copy(vbuf, vsend, vrecv, zz, c).start()
+        norm_rope(q_scale, gains.at[0], qbuf.at[zz])
 
     own_x.wait()
     own_p.wait()
-    for cp in w_copies[:3]:
+    for cp in w_copies:
         cp.wait()
 
-    def phase1(t, carry):
-        zz = src_z(t)
-
-        @pl.when(t > 0)
-        def _():
-            p_copy(z, zz).wait_recv()
-            x_copy(z, zz).wait_recv()
-        qkv_block(zz)
-        return carry
-    lax.fori_loop(0, n_z, phase1, 0)
-
-    w_copies[3].wait()
-
-    def kv_wait(zz, carry):
-        kv_copy(kbuf, ksend, krecv, zz, 1 - c).wait_recv()
-        kv_copy(vbuf, vsend, vrecv, zz, 1 - c).wait_recv()
-        return carry
-    lax.fori_loop(0, n_z, kv_wait, 0)
 
     keys = CORES * seq_loc
     lim = SCALE * LOG2E
@@ -221,20 +231,45 @@
 
     own_y = pltpu.make_async_copy(xbuf.at[z], y_ref.at[z], yrecv.at[z])
 
-    def phase2(u, carry):
-        zz = src_z(n_z - 1 - u)
-        attend(zz)
-        out_block(zz)
-
-        @pl.when(u < n_z - 1)
+    def step(i, done):
+        code = code_at(STEPS, i)
+        zz = (z + code) % n_z
+
+        @pl.when(code < n_z)
         def _():
-            y_copy(zz, z).start()
-        return carry
-    lax.fori_loop(0, n_z, phase2, 0)
-    own_y.start()
+            @pl.when(code > 0)
+            def _():
+                p_copy(z, zz).wait_recv()
+                x_copy(z, zz).wait_recv()
+            qkv_block(zz)
+
+        @pl.when(code >= n_z)
+        def _():
+            def kv_wait(j, carry):
+                prev = code_at(STEPS, j)
+
+                @pl.when(prev < n_z)
+                def _():
+                    src = (z + prev) % n_z
+                    kv_copy(kbuf, ksend, krecv, src, 1 - c).wait_recv()
+                    kv_copy(vbuf, vsend, vrecv, src, 1 - c).wait_recv()
+                return carry
+            lax.fori_loop(done, i, kv_wait, 0)
+            attend(zz)
+            out_block(zz)
+
+            @pl.when(code > n_z)
+            def _():
+                y_copy(zz, z).start()
+
+            @pl.when(code == n_z)
+            def _():
+                own_y.start()
+        return jnp.where(code < n_z, done, i)
+    lax.fori_loop(0, 2 * n_z, step, 0)
 
     def drain(t, carry):
-        zz = src_z(t)
+        zz = (z + t) % n_z
         p_copy(zz, z).wait_send()
         x_copy(zz, z).wait_send()
         y_copy(zz, z).wait_send()
@@ -248,6 +283,19 @@
         return carry
     lax.fori_loop(0, n_z, kv_drain, 0)
     own_y.wait()
+
+
+def copy_kernel(src_ref, dst_ref, buf, in_sem, out_sem):
+    parts = src_ref.shape[0]
+    reads = [pltpu.make_async_copy(src_ref.at[i], buf.at[i], in_sem.at[i]) for i in range(parts)]
+    writes = [pltpu.make_async_copy(buf.at[i], dst_ref.at[i], out_sem.at[i]) for i in range(parts)]
+    for cp in reads:
+        cp.start()
+    for rd, wr in zip(reads, writes):
+        rd.wait()
+        wr.start()
+    for cp in writes:
+        cp.wait()
 
 
 def solution(mesh):
@@ -261,7 +309,7 @@
         any_spec = pl.BlockSpec(memory_space=pl.ANY)
         vmem = pl.BlockSpec(memory_space=pltpu.VMEM)
         dma = pltpu.SemaphoreType.DMA
-        return pl.pallas_call(
+        y_home = pl.pallas_call(
             functools.partial(block_kernel, n_z),
             out_shape=jax.ShapeDtypeStruct(x_loc.shape, BF),
             in_specs=[any_spec] * 6 + [vmem] * 4,
@@ -281,6 +329,13 @@
             ] + [dma((n_z,))] * 10,
             compiler_params=pltpu.CompilerParams(collective_id=0, has_side_effects=True, vmem_limit_bytes=67043328),
         )(x_loc, pos_loc[:, None, :], w_query, w_key, w_value, w_out, freq, gain_q, gain_k, gain_out)
+        return pl.pallas_call(
+            copy_kernel,
+            out_shape=jax.ShapeDtypeStruct(x_loc.shape, BF),
+            in_specs=[any_spec],
+            out_specs=any_spec,
+            scratch_shapes=[pltpu.VMEM(x_loc.shape, BF), dma((batch,)), dma((batch,))],
+        )(y_home)
 
     tok_spec = P('dp', 'sp', None)
     return jax.shard_map(local_block, mesh=mesh, in_specs=(tok_spec, P('dp', 'sp'), P(), P(), P(), P(), P(), P(), P()), out_specs=tok_spec, check_vma=False)

time: 226 us -> 223 us (0.987)
  local copies, waits for them, and re-layouts: 4.79 us -> 0 us
    unnamed x1 -> x0, local copies, waits for them, and re-layouts: 4.79 us -> none
    pallas_call x0 -> x1, Pallas kernels: none -> 3.58 us  [local_block(): pl.pallas_call(copy_kernel, out_shape=jax.ShapeDtypeStruct(x_loc.shape, B...]
    pallas_call x1, Pallas kernels: 221 us -> 219 us  [local_block(): pl.pallas_call(functools.partial(block_kernel, n_z), out_shape=jax.ShapeD...]
where the time goes in v3:
time: 223 us
  Pallas kernels  223 us (100%)
    pallas_call x1, Pallas kernels, local_block(): pl.pallas_call(functools.partial(block_kernel, n_z), out_shape=jax.ShapeD...  219 us

profile of v3, /device:TPU:21, one launch (start us, length us, event | category | flops | bytes accessed | tf_op | source)
XLA Modules:
  0.0 222.6 jit_solution(18380839229202576788)
XLA Ops:
  0.0 219.0 %shard_map.100.src_ref = bf16[8,128,2048]{2,1,0:T(8,128)(2,1)} custom-call(bf16[8,128,2048]{2,1,0:T(8,128)(2,1)} %x_ref.1, s32[8,1,128]{2,1,0:T(1,128)} %bitcast.1, bf16[2048,2048]{1,0:T(8,128)(2,1)} %wq_ref.1, bf16[2048,2048]{1,0:T(8,128)(2,1)} %wk_ref.1, bf16[2048,2048]{1,0:T(8,128)(2,1)} %wv_ref.1, bf16[2048,2048]{1,0:T(8,128)(2,1)} %wo_ref.1, ...), custom_call_target="tpu_custom_call" | custom-call | tf_op jit(solution)/shard_map/pallas_call | solution.py:312
  219.0 3.6 %shard_map.101 = bf16[8,128,2048]{2,1,0:T(8,128)(2,1)} custom-call(bf16[8,128,2048]{2,1,0:T(8,128)(2,1)} %shard_map.100.src_ref), custom_call_target="tpu_custom_call" | custom-call | tf_op jit(solution)/shard_map/pallas_call | solution.py:332

commit v4 on v3

--- a/solution.py
+++ b/solution.py
@@ -33,14 +33,14 @@
     [1, 7, 2, 6, 3, 5, 4],
 ]
 STEPS = [
-    [0, 1, 6, 3, 2, 5, 10, 4, 12, 13, 7, 11, 9, 14, 8, 15],
-    [0, 7, 6, 2, 8, 5, 3, 1, 4, 12, 10, 9, 14, 13, 11, 15],
-    [0, 7, 2, 1, 6, 5, 9, 3, 4, 12, 8, 11, 14, 13, 10, 15],
-    [0, 1, 7, 2, 6, 5, 13, 3, 11, 4, 12, 9, 14, 8, 15, 10],
-    [0, 5, 4, 12, 2, 7, 1, 6, 8, 9, 15, 3, 10, 13, 14, 11],
-    [0, 3, 2, 11, 1, 4, 12, 5, 7, 13, 6, 9, 15, 10, 14, 8],
-    [0, 6, 3, 1, 2, 11, 4, 12, 5, 7, 13, 9, 8, 10, 15, 14],
-    [0, 2, 7, 3, 1, 5, 4, 12, 11, 6, 15, 9, 10, 14, 8, 13],
+    [0, 1, 9, 2, 7, 10, 3, 8, 5, 6, 4, 13, 15, 11, 12, 14],
+    [0, 1, 2, 7, 3, 15, 9, 4, 12, 6, 5, 13, 14, 10, 8, 11],
+    [0, 2, 7, 1, 6, 3, 11, 5, 4, 13, 9, 14, 10, 8, 15, 12],
+    [0, 1, 7, 6, 5, 2, 3, 14, 13, 11, 4, 9, 15, 10, 12, 8],
+    [0, 7, 5, 2, 4, 1, 6, 9, 15, 14, 3, 12, 11, 8, 13, 10],
+    [0, 7, 2, 6, 3, 5, 1, 11, 4, 14, 12, 10, 9, 8, 15, 13],
+    [0, 7, 6, 1, 4, 2, 10, 3, 5, 12, 13, 9, 8, 11, 15, 14],
+    [0, 1, 3, 2, 6, 5, 4, 12, 13, 11, 9, 7, 10, 14, 8, 15],
 ]
 
 

time: 223 us -> 216 us (0.969)
  Pallas kernels: 223 us -> 215 us
    pallas_call x1, Pallas kernels: 219 us -> 212 us  [local_block(): pl.pallas_call(functools.partial(block_kernel, n_z), out_shape=jax.ShapeD...]
where the time goes in v4:
time: 216 us; the launch traced here: 215 us
  Pallas kernels  215 us (100%)
    pallas_call x1, Pallas kernels, local_block(): pl.pallas_call(functools.partial(block_kernel, n_z), out_shape=jax.ShapeD...  212 us

profile of v4, /device:TPU:21, one launch (start us, length us, event | category | flops | bytes accessed | tf_op | source)
XLA Modules:
  0.0 215.2 jit_solution(17586574616146046150)
XLA Ops:
  0.0 211.6 %shard_map.100.src_ref = bf16[8,128,2048]{2,1,0:T(8,128)(2,1)} custom-call(bf16[8,128,2048]{2,1,0:T(8,128)(2,1)} %x_ref.1, s32[8,1,128]{2,1,0:T(1,128)} %bitcast.1, bf16[2048,2048]{1,0:T(8,128)(2,1)} %wq_ref.1, bf16[2048,2048]{1,0:T(8,128)(2,1)} %wk_ref.1, bf16[2048,2048]{1,0:T(8,128)(2,1)} %wv_ref.1, bf16[2048,2048]{1,0:T(8,128)(2,1)} %wo_ref.1, ...), custom_call_target="tpu_custom_call" | custom-call | tf_op jit(solution)/shard_map/pallas_call | solution.py:312
  211.6 3.6 %shard_map.101 = bf16[8,128,2048]{2,1,0:T(8,128)(2,1)} custom-call(bf16[8,128,2048]{2,1,0:T(8,128)(2,1)} %shard_map.100.src_ref), custom_call_target="tpu_custom_call" | custom-call | tf_op jit(solution)/shard_map/pallas_call | solution.py:332
